TPU v7x, 32 devices: a whole 2x2x4 slice. The times are simulated.
32 devices in a mesh: tm: 4 (over y, x), space: 8 (over z, core).
Axes of the slice: x: 2, y: 2, z: 4, core: 2. Of those that a mesh axis runs over, the one named last changes fastest.
Arguments:
- residual_field: float32 [64, 128, 128, 128], P('tm', 'space'), may hold values from -6 to 6
- eigvec_x: float32 [128, 128], replicated, may hold values from -1 to 1, as said below
- eigvec_y: float32 [128, 128], replicated, may hold values from -1 to 1, as said below
- eigvec_z: float32 [128, 128], replicated, may hold values from -1 to 1, as said below
- eigval_x: float32 [128], replicated, may hold values from 0.0001 to 0.05
- eigval_y: float32 [128], replicated, may hold values from 0.0001 to 0.05
- eigval_z: float32 [128], replicated, may hold values from 0.0001 to 0.05
Outputs:
- update: float32 [64, 128, 128, 128], P('tm', 'space')
Inputs may be any that keep to these rules, and one draw needn't show every extreme that they name: `eigvec_x`: an orthogonal matrix. `eigvec_y`: an orthogonal matrix. `eigvec_z`: an orthogonal matrix.
All inputs are finite; a program needn't handle non-finite values.
Results may differ from a plain program's by a relative error of at most 0.00025.
Values sent between devices are 32-bit elements; how exact they have to be, the bound alone decides.
A program may use at most 256 MiB of HBM per device.

v0:
```python
import jax
import jax.numpy as jnp
from jax import lax
from jax.sharding import PartitionSpec as P

highest = lax.Precision.HIGHEST
circulant_alpha = 0.01


def entering(part, axis, combine, identity):
    place = lax.axis_index(axis)
    gathered = jax.tree.map(lambda a: lax.all_gather(a, axis), part)
    state = jax.tree.map(lambda a, e: jnp.zeros_like(a) + jnp.asarray(e, a.dtype), part, identity)

    def one(step, state):
        return combine(
            state, jax.tree.map(lambda a: lax.dynamic_index_in_dim(a, step, 0, False), gathered)
        )

    return lax.fori_loop(0, place, one, state)


def recurrence_solve(values, shifts, time_count):
    steps_local = values.shape[0]
    damping = 1.0 / (1.0 + shifts)

    def advance(running, step_row):
        running = damping * (running + step_row)
        return (running, running)

    final_state, partial_value = lax.scan(advance, jnp.zeros_like(shifts), values)
    block_decay = damping**steps_local
    position = lax.axis_index("tm")

    def compose(early_map, late_map):
        return (early_map[0] * late_map[0], late_map[0] * early_map[1] + late_map[1])

    lead_power, offset = entering(
        (block_decay, final_state), "tm", compose, (jnp.ones_like(shifts), jnp.zeros_like(shifts))
    )
    tail_power = jnp.power(block_decay, (time_count - 1 - position).astype(jnp.float32))
    overall = lax.psum(tail_power * final_state, "tm")
    start_value = circulant_alpha * overall / (1.0 - circulant_alpha * block_decay**time_count)
    incoming = lead_power * start_value + offset
    exponents = jnp.arange(1, steps_local + 1, dtype=jnp.int32).astype(jnp.float32)
    powers = jnp.power(damping[None], exponents[:, None, None])
    return partial_value + powers * incoming[None]


def shards(residual_field, eigvec_x, eigvec_y, eigvec_z, eigval_x, eigval_y, eigval_z):
    steps_local, rows_x, size_y, size_z = residual_field.shape
    space_count = lax.axis_size("space")
    time_count = lax.axis_size("tm")
    planes = jnp.einsum("txyz,zk->txyk", residual_field, eigvec_z, precision=highest)
    planes = jnp.einsum("txyk,yj->txjk", planes, eigvec_y, precision=highest)
    planes = planes.reshape(steps_local, rows_x, size_y * size_z)
    x_lines = lax.all_to_all(planes, "space", split_axis=2, concat_axis=1, tiled=True)
    x_lines = jnp.einsum("txm,xi->tim", x_lines, eigvec_x, precision=highest)
    band_rows = size_y // space_count
    y_start = lax.axis_index("space") * band_rows
    shift_y = lax.dynamic_slice_in_dim(eigval_y, y_start, band_rows, 0)
    shift_yz = (shift_y[:, None] + eigval_z[None, :]).reshape(band_rows * size_z)
    shifts = eigval_x[:, None] + shift_yz[None, :]
    x_lines = recurrence_solve(x_lines, shifts, time_count)
    x_lines = jnp.einsum("tim,xi->txm", x_lines, eigvec_x, precision=highest)
    planes = lax.all_to_all(x_lines, "space", split_axis=1, concat_axis=2, tiled=True)
    planes = planes.reshape(steps_local, rows_x, size_y, size_z)
    planes = jnp.einsum("txjk,yj->txyk", planes, eigvec_y, precision=highest)
    return jnp.einsum("txyk,zk->txyz", planes, eigvec_z, precision=highest)


def solution(mesh):
    placed = (P("tm", "space", None, None), P(), P(), P(), P(), P(), P())
    return jax.shard_map(
        shards, mesh=mesh, in_specs=placed, out_specs=P("tm", "space", None, None), check_vma=False
    )
```

profile of v0, /device:TPU:9, one launch (start us, length us, event | category | flops | bytes accessed | tf_op | source)
XLA Modules:
  0.0 1588.4 jit_solution(9850415541593090977)
XLA Ops:
  6.5 22.2 %fusion.19 = f32[16,16,128,128]{2,3,1,0:T(8,128)} fusion(f32[16,16,128,128]{3,2,1,0:T(8,128)} %param.11, f32[128,128]{1,0:T(8,128)} %param.14), kind=kOutput, calls=%fused_computation.29 | convolution fusion | flops 6442450944 | bytes 33619968 | tf_op jit(solution)/shard_map/txyz,zk->txyk/dot_general | solution.py:54
  28.7 18.3 %convolution_bitcast_fusion = f32[16,16,128,128]{2,3,1,0:T(8,128)} fusion(f32[16,16,128,128]{2,3,1,0:T(8,128)} %fusion.19, f32[128,128]{1,0:T(8,128)S(1)} %copy-done.2), kind=kOutput, calls=%fused_computation.14 | convolution fusion | flops 6442450944 | bytes 33619968 | tf_op jit(solution)/shard_map/txyk,yj->txjk/dot_general | solution.py:55
  47.0 97.5 %copy.37 = f32[16,16,128,128]{1,0,3,2:T(8,128)} copy(f32[16,16,128,128]{2,3,1,0:T(8,128)} %convolution_bitcast_fusion) | data formatting | bytes 33554432 | tf_op jit(solution)/shard_map/reshape | solution.py:56
  144.5 105.2 %reshape.117 = f32[8,1,524288]{2,1,0:T(1,128)} reshape(f32[16384,16,16]{2,1,0:T(8,128)} %bitcast.55) | data formatting | bytes 33554432
  249.6 5.8 all-to-all-start
  257.1 358.4 %all-to-all-done = f32[8,1,524288]{2,1,0:T(1,128)} async-done(((f32[8,1,524288]{2,1,0:T(1,128)}), f32[8,1,524288]{2,1,0:T(1,128)}, u32[]{:S(2)}, u32[]{:S(2)}) %all-to-all-start) | async-done | bytes 16777248 | tf_op jit(solution)/shard_map/all_to_all | solution.py:57
  616.0 50.2 %reduce = f32[8,524288]{1,0:T(8,128)} reduce(f32[8,1,524288]{2,1,0:T(1,128)} %all-to-all-done, f32[]{:T(128)} %broadcast.127), dimensions={1}, to_apply=%all_to_all.24.reduce_sub_computation | reduce | bytes 33554436 | tf_op jit(solution)/shard_map/all_to_all | solution.py:57
  666.2 112.8 %reshape.118 = f32[16384,16,16]{2,1,0:T(8,128)} reshape(f32[8,524288]{1,0:T(8,128)} %reduce) | data formatting | bytes 33554432
  778.9 78.9 %copy.21 = f32[16,8,16,2048]{3,2,1,0:T(8,128)} copy(f32[16,8,16,2048]{2,0,3,1:T(8,128)} %bitcast.10) | data formatting | bytes 33554432 | tf_op jit(solution)/shard_map/all_to_all | solution.py:57
  857.8 30.9 %convolution_bitcast_fusion.1 = f32[16,128,2048]{1,2,0:T(8,128)} fusion(f32[16,128,2048]{2,1,0:T(8,128)} %bitcast.68, f32[128,128]{1,0:T(8,128)S(1)} %copy-done), kind=kOutput, calls=%fused_computation.19 | convolution fusion | flops 6442450944 | bytes 33619968 | tf_op jit(solution)/shard_map/txm,xi->tim/dot_general | solution.py:58
  888.7 50.7 %while.26 = (s32[]{:T(128)}, f32[128,2048]{1,0:T(8,128)S(1)}, f32[16,128,2048]{2,1,0:T(8,128)}, f32[16,128,2048]{1,2,0:T(8,128)}, f32[2048]{0:T(1024)S(1)}, /*index=5*/f32[128]{0:T(128)S(1)}, s32[]{:T(128)}, s32[]{:T(128)}) while((s32[]{:T(128)}, f32[128,2048]{1,0:T(8,128)S(1)}, f32[16,128,2048]{2,1,0:T(8,128)}, ...), condition=%wide.region_1.2_spmd.clone, body=%wide.region_0.1_spmd.clone.sunk | while | flops 1572867 | bytes 8397923 | solution.py:31
  888.7 1.3 constant_dynamic-slice_fusion.2
  890.3 1.5 bitcast_dynamic-update-slice_fusion.2
  891.9 1.3 constant_dynamic-slice_fusion.2
  893.5 1.5 bitcast_dynamic-update-slice_fusion.2
  895.0 1.3 constant_dynamic-slice_fusion.2
  896.7 1.5 bitcast_dynamic-update-slice_fusion.2
  898.2 1.3 constant_dynamic-slice_fusion.2
  899.8 1.5 bitcast_dynamic-update-slice_fusion.2
  901.4 1.3 constant_dynamic-slice_fusion.2
  903.0 1.5 bitcast_dynamic-update-slice_fusion.2
  904.5 1.3 constant_dynamic-slice_fusion.2
  906.2 1.5 bitcast_dynamic-update-slice_fusion.2
  907.7 1.3 constant_dynamic-slice_fusion.2
  909.4 1.5 bitcast_dynamic-update-slice_fusion.2
  910.9 1.3 constant_dynamic-slice_fusion.2
  912.5 1.5 bitcast_dynamic-update-slice_fusion.2
  915.7 1.5 bitcast_dynamic-update-slice_fusion.2
  917.2 1.3 constant_dynamic-slice_fusion.2
  918.9 1.5 bitcast_dynamic-update-slice_fusion.2
  922.0 1.5 bitcast_dynamic-update-slice_fusion.2
  925.2 1.5 bitcast_dynamic-update-slice_fusion.2
  926.7 1.3 constant_dynamic-slice_fusion.2
  928.4 1.5 bitcast_dynamic-update-slice_fusion.2
  931.5 1.5 bitcast_dynamic-update-slice_fusion.2
  934.7 1.5 bitcast_dynamic-update-slice_fusion.2
  937.9 1.5 bitcast_dynamic-update-slice_fusion.2
  940.5 3.6 add_divide_fusion
  944.2 51.3 %all-gather.6.cloned.1.call-done = f32[512,2048]{1,0:T(8,128)} async-done(((f32[128,2048]{1,0:T(8,128)}), f32[512,2048]{1,0:T(8,128)}) %all-gather.6.cloned.1.call-update) | async-done | bytes 4194320 | tf_op jit(solution)/shard_map/all_gather | solution.py:12
  995.7 55.3 %all-reduce.2.cloned.1.call-done = f32[128,2048]{1,0:T(8,128)} async-done(((f32[128,2048]{1,0:T(8,128)}), f32[128,2048]{1,0:T(8,128)}) %all-reduce.2.cloned.1.call-update) | async-done | bytes 1048592 | tf_op jit(solution)/shard_map/psum | solution.py:42
  1051.1 1.8 multiply_add_fusion
  1052.9 47.1 %fusion.12 = f32[16,128,2048]{1,2,0:T(8,128)} fusion(f32[16,128,2048]{2,1,0:T(8,128)} %get-tuple-element.67, f32[128,2048]{1,0:T(8,128)S(1)} %multiply_add_fusion, f32[16]{0:T(128)S(1)} %add_convert_fusion, f32[128,2048]{1,0:T(8,128)S(1)} %get-tuple-element.142, f32[128,128]{1,0:T(8,128)S(1)} %copy-done), kind=kOutput, calls=%fused_computation.18 | convolution fusion | flops 6450839552 | bytes 35717184 | tf_op jit(solution)/shard_map/tim,xi->txm/dot_general | solution.py:65
  1100.0 18.2 %copy.25 = f32[16,128,2048]{2,0,1:T(8,128)} copy(f32[16,128,2048]{1,2,0:T(8,128)} %fusion.12) | data formatting | bytes 33554432 | tf_op jit(solution)/shard_map/tim,xi->txm/transpose | solution.py:65
  1118.2 367.2 %all_to_all.33 = f32[16,128,2048]{2,0,1:T(8,128)S(1)} all-to-all(f32[16,128,2048]{2,0,1:T(8,128)} %copy.25), channel_id=1, replica_groups=mesh['tm'=4,'space'=8] {'space'}, dimensions={1} | all-to-all | bytes 33554432 | tf_op jit(solution)/shard_map/all_to_all | solution.py:66
  1485.4 18.4 %copy.27 = f32[16,16,8,2048]{3,2,1,0:T(8,128)} copy(f32[16,16,8,2048]{3,0,1,2:T(8,128)S(1)} %bitcast.69) | data formatting | bytes 33554432 | tf_op jit(solution)/shard_map/all_to_all | solution.py:66
  1503.9 18.0 %reshape.112 = f32[16,16,128,128]{3,2,1,0:T(8,128)} reshape(f32[16,16,8,2048]{3,2,1,0:T(8,128)} %copy.27) | data formatting | bytes 33554432 | tf_op jit(solution)/shard_map/reshape | solution.py:67
  1521.9 29.8 %fusion.15 = f32[16,16,128,128]{3,2,1,0:T(8,128)S(1)} fusion(f32[16,16,128,128]{3,2,1,0:T(8,128)} %reshape.112, f32[128,128]{1,0:T(8,128)S(1)} %copy-done.3), kind=kOutput, calls=%fused_computation.25 | convolution fusion | flops 6442450944 | bytes 33619968 | tf_op jit(solution)/shard_map/txjk,yj->txyk/dot_general | solution.py:68
  1551.7 29.8 %fusion.3 = f32[16,16,128,128]{3,2,1,0:T(8,128)} fusion(f32[16,16,128,128]{3,2,1,0:T(8,128)S(1)} %fusion.15, f32[128,128]{1,0:T(8,128)S(1)} %copy-done.4), kind=kOutput, calls=%fused_computation.8 | convolution fusion | flops 6442450944 | bytes 33619968 | tf_op jit(solution)/shard_map/txyk,zk->txyz/dot_general | solution.py:69
  (55 shorter events, 16.4 us)
Async XLA Ops:
  6.5 851.3 %copy-start = (f32[128,128]{1,0:T(8,128)S(1)}, f32[128,128]{1,0:T(8,128)}, u32[]{:S(2)}) copy-start(f32[128,128]{1,0:T(8,128)} %param.12) | copy-start | bytes 196612
  6.5 22.2 %copy-start.2 = (f32[128,128]{1,0:T(8,128)S(1)}, f32[128,128]{1,0:T(8,128)}, u32[]{:S(2)}) copy-start(f32[128,128]{1,0:T(8,128)} %param.13) | copy-start | bytes 196612
  249.6 5.9 copy-start.7
  249.6 6.0 copy-start.6
  249.6 6.1 copy-start.5
  249.6 365.8 %all-to-all-start = ((f32[8,1,524288]{2,1,0:T(1,128)}), f32[8,1,524288]{2,1,0:T(1,128)}, u32[]{:S(2)}, u32[]{:S(2)}) async-start(f32[8,1,524288]{2,1,0:T(1,128)} %reshape.117), calls=%async_computation | async-start | bytes 33554432 | tf_op jit(solution)/shard_map/all_to_all | solution.py:57
  255.5 688.6 %all-gather.4.cloned.1.call-start = ((), (), s32[]{:S(2)}) async-start(), calls=%async_computation.2 | async-start | bytes 5242880 | tf_op jit(solution)/shard_map/all_gather | solution.py:12
  257.0 738.5 %all-gather.6.cloned.1.call-start = ((), (), s32[]{:S(2)}) async-start(), calls=%async_computation.4 | async-start | bytes 5242880 | tf_op jit(solution)/shard_map/all_gather | solution.py:12
  939.4 1.0 copy-start.1
  940.4 110.6 %all-reduce.2.cloned.1.call-start = ((), (), s32[]{:S(2)}) async-start(), calls=%async_computation.3 | async-start | bytes 2097152 | tf_op jit(solution)/shard_map/psum | solution.py:42
  1503.9 18.0 %copy-start.3 = (f32[128,128]{1,0:T(8,128)S(1)}, f32[128,128]{1,0:T(8,128)}, u32[]{:S(2)}) copy-start(f32[128,128]{1,0:T(8,128)} %param.13) | copy-start | bytes 196612
  1521.9 29.8 %copy-start.4 = (f32[128,128]{1,0:T(8,128)S(1)}, f32[128,128]{1,0:T(8,128)}, u32[]{:S(2)}) copy-start(f32[128,128]{1,0:T(8,128)} %param.14) | copy-start | bytes 196612
Sparse Core Ops, SparseCore 0:
  258.2 53.6 all-gather.3
  940.5 54.8 all-gather.5
  998.6 52.4 all-reduce.1
where the time goes:
time: 1600 us; the launch traced here: 1590 us
  local copies, waits for them, and re-layouts  477 us (30%)
  waiting for transfers between devices  465 us (29%)
  blocking collectives  367 us (23%)
  matrix products  178 us (11%)
  other arithmetic  81.5 us (5%)
    all_to_all x1, blocking collectives, shards(): lax.all_to_all(x_lines, 'space', split_axis=1, concat_axis=2, tiled=True)  367 us
    all_to_all x1, waiting for transfers between devices, shards(): lax.all_to_all(planes, 'space', split_axis=2, concat_axis=1, tiled=True)  358 us
    unnamed x18, local copies, waits for them, and re-layouts  219 us
    reshape x1, local copies, waits for them, and re-layouts, shards(): planes = planes.reshape(steps_local, rows_x, size_y * size_z)  97.5 us
    all_to_all x2, local copies, waits for them, and re-layouts, shards(): lax.all_to_all(planes, 'space', split_axis=2, concat_axis=1, tiled=True)  79.3 us
    psum x1, waiting for transfers between devices, recurrence_solve(): overall = lax.psum(tail_power * final_state, 'tm')  55.3 us
    all_gather x2, waiting for transfers between devices, entering(): gathered = jax.tree.map(lambda a: lax.all_gather(a, axis), part)  51.4 us
    all_to_all x1, other arithmetic, shards(): lax.all_to_all(planes, 'space', split_axis=2, concat_axis=1, tiled=True)  50.2 us
  transfers between devices with their start and end apart: 4, of which 3 were waited for; matrix products, arithmetic and copies ran while one was open for 21% of the time, Pallas kernels for 0%

commit v1 on v0

--- a/solution.py
+++ b/solution.py
@@ -1,10 +1,277 @@
+import functools
 import jax
 import jax.numpy as jnp
 from jax import lax
+from jax.experimental import pallas as pl
+from jax.experimental.pallas import tpu as pltpu
 from jax.sharding import PartitionSpec as P
 
 highest = lax.Precision.HIGHEST
 circulant_alpha = 0.01
+tile_rows = 8
+
+
+def halves(a):
+    high = a.astype(jnp.bfloat16)
+    return high, (a - high.astype(jnp.float32)).astype(jnp.bfloat16)
+
+
+def stacked(matrix):
+    return jnp.concatenate(halves(matrix), axis=0)
+
+
+def left_product(left, a):
+    rows, columns = left.shape[0] // 2, a.shape[1]
+    r = jnp.dot(left, jnp.concatenate(halves(a), axis=1), preferred_element_type=jnp.float32)
+    return (r[:rows, :columns] + r[rows:, :columns]) + (r[:rows, columns:] + r[rows:, columns:])
+
+
+def right_product(a, right):
+    columns = right.shape[1] // 2
+    r = jnp.dot(jnp.concatenate(halves(a), axis=1), right, preferred_element_type=jnp.float32)
+    return r[:, :columns] + r[:, columns:]
+
+
+def power(a, n):
+    result = None
+    while n:
+        if n & 1:
+            result = a if result is None else result * a
+        a, n = a * a, n >> 1
+    return result
+
+
+def plane_kernel(a_ref, left_ref, right_ref, o_ref):
+    left = stacked(left_ref[...])
+    right = jnp.concatenate(halves(right_ref[...]), axis=1)
+    right = jnp.concatenate([right, right], axis=0)
+
+    def one(x, carry):
+        o_ref[0, x] = left_product(left, right_product(a_ref[0, x], right))
+        return carry
+
+    lax.fori_loop(0, a_ref.shape[1], one, 0, unroll=4)
+
+
+def plane_transform(a, left, right):
+    steps, rows, size_y, size_z = a.shape
+    block = pl.BlockSpec((1, rows, size_y, size_z), lambda t: (t, 0, 0, 0))
+    whole = lambda m: pl.BlockSpec(m.shape, lambda t: (0, 0))
+    return pl.pallas_call(
+        plane_kernel,
+        grid=(steps,),
+        in_specs=[block, whole(left), whole(right)],
+        out_specs=block,
+        out_shape=jax.ShapeDtypeStruct(a.shape, jnp.float32),
+        compiler_params=pltpu.CompilerParams(vmem_limit_bytes=60 * 2**20),
+    )(a, left, right)
+
+
+def exchange_kernel(
+    space_count, time_count, chunks,
+    in_ref, vt_ref, v_ref, ex_ref, shift_ref, out_ref,
+    recv, fins, own_in, own_out, go_send, go_recv, back_send, back_recv, st_send, st_recv,
+):
+    steps, rows, band_rows = recv.shape[2], recv.shape[3], recv.shape[4]
+    size_z = recv.shape[5]
+    band = band_rows * chunks
+    me = lax.axis_index("space")
+    position = lax.axis_index("tm")
+
+    def peer_of(k):
+        return lax.rem(me + k, space_count)
+
+    def timer_of(k):
+        return lax.rem(position + k, time_count)
+
+    def columns(owner, c):
+        return pl.ds(pl.multiple_of(owner * band + c * band_rows, tile_rows), band_rows)
+
+    def go(c, peer):
+        return pltpu.make_async_remote_copy(
+            src_ref=in_ref.at[:, :, columns(peer, c), :],
+            dst_ref=recv.at[c, me],
+            send_sem=go_send.at[c, peer],
+            recv_sem=go_recv.at[c, me],
+            device_id={"space": peer},
+            device_id_type=pl.DeviceIdType.MESH,
+        )
+
+    def go_arrival(c, peer):
+        return pltpu.make_async_remote_copy(
+            src_ref=in_ref.at[:, :, columns(peer, c), :],
+            dst_ref=recv.at[c, peer],
+            send_sem=go_send.at[c, peer],
+            recv_sem=go_recv.at[c, peer],
+            device_id={"space": peer},
+            device_id_type=pl.DeviceIdType.MESH,
+        )
+
+    def back(c, peer):
+        return pltpu.make_async_remote_copy(
+            src_ref=recv.at[c, peer],
+            dst_ref=out_ref.at[:, :, columns(me, c), :],
+            send_sem=back_send.at[c, peer],
+            recv_sem=back_recv.at[c, me],
+            device_id={"space": peer},
+            device_id_type=pl.DeviceIdType.MESH,
+        )
+
+    def back_arrival(c, peer):
+        return pltpu.make_async_remote_copy(
+            src_ref=recv.at[c, peer],
+            dst_ref=out_ref.at[:, :, columns(peer, c), :],
+            send_sem=back_send.at[c, peer],
+            recv_sem=back_recv.at[c, peer],
+            device_id={"space": peer},
+            device_id_type=pl.DeviceIdType.MESH,
+        )
+
+    def final(c, peer, owner):
+        return pltpu.make_async_remote_copy(
+            src_ref=fins.at[c, owner],
+            dst_ref=fins.at[c, owner],
+            send_sem=st_send.at[c, peer],
+            recv_sem=st_recv.at[c, owner],
+            device_id={"tm": peer},
+            device_id_type=pl.DeviceIdType.MESH,
+        )
+
+    def take_own(c):
+        return pltpu.make_async_copy(
+            in_ref.at[:, :, columns(me, c), :], recv.at[c, me], own_in.at[c]
+        )
+
+    def give_own(c):
+        return pltpu.make_async_copy(
+            recv.at[c, me], out_ref.at[:, :, columns(me, c), :], own_out.at[c]
+        )
+
+    barrier = pltpu.get_barrier_semaphore()
+    for k in range(1, space_count):
+        pl.semaphore_signal(
+            barrier, inc=1, device_id={"space": peer_of(k)}, device_id_type=pl.DeviceIdType.MESH
+        )
+    for k in range(1, time_count):
+        pl.semaphore_signal(
+            barrier, inc=1, device_id={"tm": timer_of(k)}, device_id_type=pl.DeviceIdType.MESH
+        )
+    pl.semaphore_wait(barrier, space_count + time_count - 2)
+
+    middle = space_count // 2
+    offsets = sorted(range(1, space_count), key=lambda k: abs(k - middle))
+    for c in range(chunks):
+        for k in offsets:
+            go(c, peer_of(k)).start()
+        take_own(c).start()
+
+    left = stacked(vt_ref[...])
+    left_back = stacked(v_ref[...])
+    ex = ex_ref[...]
+
+    def load(c, t, j):
+        parts = [
+            recv.at[c, s, t].reshape(rows * band_rows, size_z)[pl.ds(j, rows, stride=band_rows), :]
+            for s in range(space_count)
+        ]
+        return jnp.concatenate(parts, axis=0)
+
+    def store(c, t, j, value):
+        for s in range(space_count):
+            view = recv.at[c, s, t].reshape(rows * band_rows, size_z)
+            view[pl.ds(j, rows, stride=band_rows), :] = value[s * rows : (s + 1) * rows]
+
+    def chunk(c, carry):
+        for k in offsets:
+            go_arrival(c, peer_of(k)).wait_recv()
+        take_own(c).wait()
+        for j in range(band_rows):
+            damping = 1.0 / (1.0 + (ex + shift_ref[c, j : j + 1, :]))
+
+            def forward(t, state, j=j, damping=damping):
+                state = damping * (state + left_product(left, load(c, t, j)))
+                store(c, t, j, state)
+                return state
+
+            fins[c, position, j] = lax.fori_loop(
+                0, steps, forward, jnp.zeros_like(damping), unroll=2
+            )
+        for k in range(1, time_count):
+            final(c, timer_of(k), position).start()
+        for k in range(1, time_count):
+            final(c, timer_of(k), timer_of(k)).wait_recv()
+        for j in range(band_rows):
+            damping = 1.0 / (1.0 + (ex + shift_ref[c, j : j + 1, :]))
+            block_decay = power(damping, steps)
+            overall = fins[c, 0, j]
+            for p in range(1, time_count):
+                overall = block_decay * overall + fins[c, p, j]
+            incoming = (circulant_alpha * overall) / (
+                1.0 - circulant_alpha * power(block_decay, time_count)
+            )
+            for p in range(time_count - 1):
+                incoming = jnp.where(
+                    p < position, block_decay * incoming + fins[c, p, j], incoming
+                )
+
+            def inverse(t, incoming, j=j, damping=damping):
+                incoming = damping * incoming
+                store(c, t, j, left_product(left_back, load(c, t, j) + incoming))
+                return incoming
+
+            lax.fori_loop(0, steps, inverse, incoming, unroll=2)
+        for k in offsets:
+            go(c, peer_of(k)).wait_send()
+            back(c, peer_of(k)).start()
+        give_own(c).start()
+        return carry
+
+    lax.fori_loop(0, chunks, chunk, 0)
+
+    for c in range(chunks):
+        for k in range(1, time_count):
+            final(c, timer_of(k), position).wait_send()
+        for k in offsets:
+            back(c, peer_of(k)).wait_send()
+            back_arrival(c, peer_of(k)).wait_recv()
+        give_own(c).wait()
+
+
+def exchange_solve(planes, eigvec_x, eigval_x, shift_yz, space_count, time_count):
+    steps, rows, size_y, size_z = planes.shape
+    band = size_y // space_count
+    chunks = 2 if band % (2 * tile_rows) == 0 else 1
+    band_rows = band // chunks
+    size_x = rows * space_count
+    vmem = pl.BlockSpec(memory_space=pltpu.VMEM)
+    dma = pltpu.SemaphoreType.DMA
+    return pl.pallas_call(
+        functools.partial(exchange_kernel, space_count, time_count, chunks),
+        in_specs=[pl.BlockSpec(memory_space=pl.ANY)] + [vmem] * 4,
+        out_specs=pl.BlockSpec(memory_space=pl.ANY),
+        out_shape=jax.ShapeDtypeStruct(planes.shape, jnp.float32),
+        scratch_shapes=[
+            pltpu.VMEM((chunks, space_count, steps, rows, band_rows, size_z), jnp.float32),
+            pltpu.VMEM((chunks, time_count, band_rows, size_x, size_z), jnp.float32),
+            dma((chunks,)),
+            dma((chunks,)),
+            dma((chunks, space_count)),
+            dma((chunks, space_count)),
+            dma((chunks, space_count)),
+            dma((chunks, space_count)),
+            dma((chunks, time_count)),
+            dma((chunks, time_count)),
+        ],
+        compiler_params=pltpu.CompilerParams(
+            collective_id=0, has_side_effects=True, vmem_limit_bytes=60 * 2**20
+        ),
+    )(
+        planes,
+        eigvec_x.T,
+        eigvec_x,
+        jnp.broadcast_to(eigval_x[:, None], (size_x, size_z)),
+        shift_yz.reshape(chunks, band_rows, size_z),
+    )
 
 
 def entering(part, axis, combine, identity):
@@ -47,26 +314,31 @@
     return partial_value + powers * incoming[None]
 
 
+def narrow_solve(planes, eigvec_x, eigval_x, shift_yz, time_count):
+    steps_local, rows_x, size_y, size_z = planes.shape
+    planes = planes.reshape(steps_local, rows_x, size_y * size_z)
+    x_lines = lax.all_to_all(planes, "space", split_axis=2, concat_axis=1, tiled=True)
+    x_lines = jnp.einsum("txm,xi->tim", x_lines, eigvec_x, precision=highest)
+    shifts = eigval_x[:, None] + shift_yz.reshape(1, -1)
+    x_lines = recurrence_solve(x_lines, shifts, time_count)
+    x_lines = jnp.einsum("tim,xi->txm", x_lines, eigvec_x, precision=highest)
+    planes = lax.all_to_all(x_lines, "space", split_axis=1, concat_axis=2, tiled=True)
+    return planes.reshape(steps_local, rows_x, size_y, size_z)
+
+
 def shards(residual_field, eigvec_x, eigvec_y, eigvec_z, eigval_x, eigval_y, eigval_z):
     steps_local, rows_x, size_y, size_z = residual_field.shape
     space_count = lax.axis_size("space")
     time_count = lax.axis_size("tm")
-    planes = jnp.einsum("txyz,zk->txyk", residual_field, eigvec_z, precision=highest)
-    planes = jnp.einsum("txyk,yj->txjk", planes, eigvec_y, precision=highest)
-    planes = planes.reshape(steps_local, rows_x, size_y * size_z)
-    x_lines = lax.all_to_all(planes, "space", split_axis=2, concat_axis=1, tiled=True)
-    x_lines = jnp.einsum("txm,xi->tim", x_lines, eigvec_x, precision=highest)
-    band_rows = size_y // space_count
-    y_start = lax.axis_index("space") * band_rows
-    shift_y = lax.dynamic_slice_in_dim(eigval_y, y_start, band_rows, 0)
-    shift_yz = (shift_y[:, None] + eigval_z[None, :]).reshape(band_rows * size_z)
-    shifts = eigval_x[:, None] + shift_yz[None, :]
-    x_lines = recurrence_solve(x_lines, shifts, time_count)
-    x_lines = jnp.einsum("tim,xi->txm", x_lines, eigvec_x, precision=highest)
-    planes = lax.all_to_all(x_lines, "space", split_axis=1, concat_axis=2, tiled=True)
-    planes = planes.reshape(steps_local, rows_x, size_y, size_z)
-    planes = jnp.einsum("txjk,yj->txyk", planes, eigvec_y, precision=highest)
-    return jnp.einsum("txyk,zk->txyz", planes, eigvec_z, precision=highest)
+    planes = plane_transform(residual_field, eigvec_y.T, eigvec_z)
+    band = size_y // space_count
+    shift_y = lax.dynamic_slice_in_dim(eigval_y, lax.axis_index("space") * band, band, 0)
+    shift_yz = shift_y[:, None] + eigval_z[None, :]
+    if band % tile_rows == 0 and rows_x % tile_rows == 0:
+        planes = exchange_solve(planes, eigvec_x, eigval_x, shift_yz, space_count, time_count)
+    else:
+        planes = narrow_solve(planes, eigvec_x, eigval_x, shift_yz, time_count)
+    return plane_transform(planes, eigvec_y, eigvec_z.T)
 
 
 def solution(mesh):

time: 1600 us -> 821 us (0.51)
  Pallas kernels: 0 us -> 815 us
  local copies, waits for them, and re-layouts: 477 us -> 4.53 us
  waiting for transfers between devices: 465 us -> 0 us
  blocking collectives: 367 us -> 0 us
  matrix products: 178 us -> 0 us
  other arithmetic: 81.5 us -> 1.33 us
    pallas_call x0 -> x3, Pallas kernels: none -> 815 us  [the longest x1 726 us: exchange_solve(): pl.pallas_call(functools.partial(exchange_kernel, space_count, time_count...]
    all_to_all x1 -> x0, blocking collectives: 367 us -> none  [shards(): lax.all_to_all(x_lines, 'space', split_axis=1, concat_axis=2, tiled=True)]
    all_to_all x1 -> x0, waiting for transfers between devices: 358 us -> none  [shards(): lax.all_to_all(planes, 'space', split_axis=2, concat_axis=1, tiled=True)]
    unnamed x18 -> x9, local copies, waits for them, and re-layouts: 219 us -> 3 us
    dot_general x6 -> x0, matrix products: 178 us -> none  [the longest x1 47.1 us: shards(): x_lines = jnp.einsum('tim,xi->txm', x_lines, eigvec_x, precision=highest)]
    reshape x2 -> x0, local copies, waits for them, and re-layouts: 115 us -> none  [the longest x1 97.5 us: shards(): planes = planes.reshape(steps_local, rows_x, size_y * size_z)]
    all_to_all x3 -> x0, local copies, waits for them, and re-layouts: 97.8 us -> none  [the longest x2 79.3 us: shards(): lax.all_to_all(planes, 'space', split_axis=2, concat_axis=1, tiled=True)]
    psum x1 -> x0, waiting for transfers between devices: 55.3 us -> none  [recurrence_solve(): overall = lax.psum(tail_power * final_state, 'tm')]
  transfers between devices with their start and end apart: 4 -> 0, of which waited for: 3 -> 0; matrix products, arithmetic and copies ran while one was open for 21% -> 0% of each run, Pallas kernels for 0% -> 0%
where the time goes in v1:
time: 821 us; the launch traced here: 820 us
  Pallas kernels  815 us (99%)
    pallas_call x1, Pallas kernels, exchange_solve(): pl.pallas_call(functools.partial(exchange_kernel, space_count, time_count...  726 us
    pallas_call x2, Pallas kernels, plane_transform(): pl.pallas_call(plane_kernel, grid=(steps,), in_specs=[block, whole(left),...  88.9 us

profile of v1, /device:TPU:9, one launch (start us, length us, event | category | flops | bytes accessed | tf_op | source)
XLA Modules:
  0.0 820.4 jit_solution(10424495069124511891)
XLA Ops:
  0.0 0.7 dynamic_slice.3
  0.7 0.1 add.20
  0.8 1.3 broadcast_add_fusion.shift_ref
  2.1 1.6 copy.8
  3.7 0.0 copy-start
  3.7 0.0 copy-start.2
  3.7 44.5 %shard_map.73.in_ref = f32[16,16,128,128]{3,2,1,0:T(8,128)} custom-call(f32[16,16,128,128]{3,2,1,0:T(8,128)} %a_ref.1, f32[128,128]{1,0:T(8,128)} %bitcast.5, f32[128,128]{1,0:T(8,128)} %right_ref.1), custom_call_target="tpu_custom_call" | custom-call | tf_op jit(solution)/shard_map/pallas_call | solution.py:60
  48.2 0.0 copy-done
  48.2 0.7 copy.9
  48.9 0.0 copy-done.2
  48.9 0.7 broadcast_in_dim.2.ex_ref
  49.6 0.0 copy-start.1
  49.6 725.7 %shard_map.74.a_ref = f32[16,16,128,128]{3,2,1,0:T(8,128)} custom-call(f32[16,16,128,128]{3,2,1,0:T(8,128)} %shard_map.73.in_ref, f32[128,128]{1,0:T(8,128)} %bitcast.3, f32[128,128]{1,0:T(8,128)} %v_ref.1, f32[128,128]{1,0:T(8,128)} %broadcast_in_dim.2.ex_ref, f32[2,8,128]{2,1,0:T(8,128)} %broadcast_add_fusion.shift_ref), custom_call_target="tpu_custom_call" | custom-call | tf_op jit(solution)/shard_map/pallas_call | solution.py:248
  775.3 0.0 copy-done.1
  775.3 0.7 copy.10
  776.0 44.4 %shard_map.75 = f32[16,16,128,128]{3,2,1,0:T(8,128)} custom-call(f32[16,16,128,128]{3,2,1,0:T(8,128)} %shard_map.74.a_ref, f32[128,128]{1,0:T(8,128)} %left_ref.1, f32[128,128]{1,0:T(8,128)} %bitcast.4), custom_call_target="tpu_custom_call" | custom-call | tf_op jit(solution)/shard_map/pallas_call | solution.py:60
Async XLA Ops:
  3.7 44.5 %copy-start = (f32[128,128]{1,0:T(8,128)S(1)}, f32[128,128]{1,0:T(8,128)}, u32[]{:S(2)}) copy-start(f32[128,128]{1,0:T(8,128)} %v_ref.1) | copy-start | bytes 196612
  3.7 45.2 %copy-start.2 = (f32[128]{0:T(128)S(1)}, f32[128]{0:T(128)}, u32[]{:S(2)}) copy-start(f32[128]{0:T(128)} %param.11) | copy-start | bytes 1540
  49.6 725.7 %copy-start.1 = (f32[128,128]{1,0:T(8,128)S(1)}, f32[128,128]{1,0:T(8,128)}, u32[]{:S(2)}) copy-start(f32[128,128]{1,0:T(8,128)} %right_ref.1) | copy-start | bytes 196612
